TPU v7x, 32 devices: a whole 2x2x4 slice. The times are simulated.
32 devices in a mesh: section: 2 (over y), dp: 16 (over z, x, core).
Axes of the slice: x: 2, y: 2, z: 4, core: 2. Of those that a mesh axis runs over, the one named last changes fastest.
Arguments:
- inputs: bfloat16 [32, 128, 1536], P('dp'), parts along dimension 0, may hold values from -6 to 6
- w_query: bfloat16 [2, 1536, 768], P('section'), may hold values from -0.15625 to 0.15625
- w_key: bfloat16 [2, 1536, 768], P('section'), may hold values from -0.15625 to 0.15625
- w_value: bfloat16 [2, 1536, 768], P('section'), may hold values from -0.15625 to 0.15625
- w_out: bfloat16 [2, 768, 1536], P('section'), may hold values from -0.21875 to 0.21875
- mixing: float32 [2], P('section'), may hold values from 0.2 to 0.8
Outputs:
- outputs: bfloat16 [32, 128, 1536], P(('dp', 'section')), parts along dimension 0
There are 16 independent parts, one for each index of `dp`. A program takes and returns all parts, laid end to end along the dimension named above; an argument that names none is the same for every part. Nothing has to cross between parts.
All inputs are finite; a program needn't handle non-finite values.
Results may differ from a plain program's by a relative error of at most 0.023.
Values may be sent and summed in bfloat16 or wider, within the bound.
A program may use at most 128 MiB of HBM per device.

v0:
```python
import jax
import jax.numpy as jnp
from jax import lax
from jax.sharding import PartitionSpec as P

HEADS = 6


epsilon = 1e-06
score_scale = 0.12


def shifted(value, axis, steps):
    count = lax.axis_size(axis)
    first, last = (max(0, -steps), min(count, count - steps))
    return lax.ppermute(value, axis, [(source, source + steps) for source in range(first, last)])


def norm_rows(tensor):
    return tensor * lax.rsqrt(jnp.mean(tensor * tensor, axis=-1, keepdims=True) + epsilon)


def project(normed, weight):
    return jnp.dot(normed, weight, preferred_element_type=jnp.float32)


def layer_apply(hidden, w_query, w_key, w_value, w_out, mixing, first_values, first_flag):
    row_count = hidden.shape[0]
    hidden_wide = hidden.astype(jnp.float32)
    normed = norm_rows(hidden_wide).astype(jnp.bfloat16)
    queries = norm_rows(project(normed, w_query).reshape(row_count, HEADS, -1)).astype(jnp.bfloat16)
    key_rows = norm_rows(project(normed, w_key).reshape(row_count, HEADS, -1)).astype(jnp.bfloat16)
    values = project(normed, w_value)
    own_values = values.astype(jnp.bfloat16)
    blended = (mixing * values + (1.0 - mixing) * first_values.astype(jnp.float32)).astype(
        jnp.bfloat16
    )
    used_values = jnp.where(first_flag, own_values, blended).reshape(row_count, HEADS, -1)
    scores = (
        jnp.einsum("qhd,khd->hqk", queries, key_rows, preferred_element_type=jnp.float32)
        * score_scale
    )
    positions = jnp.arange(row_count, dtype=jnp.int32)
    causal = positions[:, None] >= positions[None, :]
    weights = jnp.where(causal[None, :, :], jnp.exp(scores), 0.0)
    probabilities = (weights / jnp.sum(weights, axis=-1, keepdims=True)).astype(jnp.bfloat16)
    attended = jnp.einsum(
        "hqk,khd->qhd", probabilities, used_values, preferred_element_type=jnp.float32
    )
    attended = attended.astype(jnp.bfloat16).reshape(row_count, -1)
    result = (hidden_wide + project(attended, w_out)).astype(jnp.bfloat16)
    return (result, own_values)


def body(inputs, w_query, w_key, w_value, w_out, mixing):
    section_count = lax.axis_size("section")
    section_index = lax.axis_index("section")
    micro_count, row_count, model_width = inputs.shape
    value_width = w_value.shape[2]
    step_count = micro_count + section_count - 1
    last_section = section_count - 1
    share_count = micro_count // section_count

    def run_layers(hidden, first_values):
        current = first_values
        first_flag = jnp.logical_and(section_index == 0, 0 == 0)
        hidden, own_values = layer_apply(
            hidden, w_query[0], w_key[0], w_value[0], w_out[0], mixing[0], current, first_flag
        )
        current = jnp.where(section_index == 0, own_values, current)
        return (hidden, current)

    def advance(time_step, carried):
        received, value_store, outputs = carried
        micro_index = time_step - section_index
        active = jnp.logical_and(micro_index >= 0, micro_index < micro_count)
        slot_index = jnp.clip(micro_index, 0, micro_count - 1)
        fresh_rows = lax.dynamic_index_in_dim(
            inputs, jnp.minimum(time_step, micro_count - 1), 0, keepdims=False
        )
        hidden = jnp.where(section_index == 0, fresh_rows, received)
        first_values = value_store

        def run_section(operands):
            section_rows, section_first = operands
            return run_layers(section_rows, section_first)

        def pass_through(operands):
            return operands

        result, current = lax.cond(active, run_section, pass_through, (hidden, first_values))
        previous = lax.dynamic_index_in_dim(outputs, slot_index, 0, keepdims=False)
        finished = jnp.where(
            jnp.logical_and(active, section_index == last_section), result, previous
        )
        outputs = lax.dynamic_update_index_in_dim(outputs, finished, slot_index, 0)
        received, value_store = shifted((result, current), "section", 1)
        return (received, value_store, outputs)

    value_store = jnp.zeros((row_count, value_width), jnp.bfloat16)
    received = jnp.zeros((row_count, model_width), jnp.bfloat16)
    outputs = jnp.zeros((micro_count, row_count, model_width), jnp.bfloat16)
    received, value_store, outputs = lax.fori_loop(
        0, step_count, advance, (received, value_store, outputs)
    )
    gathered = lax.all_to_all(outputs, "section", split_axis=0, concat_axis=0, tiled=True)
    return gathered[last_section * share_count :]


def solution(mesh):
    in_specs = (
        P("dp", None, None),
        P("section", None, None),
        P("section", None, None),
        P("section", None, None),
        P("section", None, None),
        P("section"),
    )
    out_specs = P(("dp", "section"), None, None)
    return jax.shard_map(body, mesh=mesh, in_specs=in_specs, out_specs=out_specs, check_vma=False)
```

profile of v0, /device:TPU:0, one launch (start us, length us, event | category | flops | bytes accessed | tf_op | source)
XLA Modules:
  0.0 114.8 jit_solution(3503634436301427195)
XLA Ops:
  0.0 2.8 %copy.17 = bf16[1,1536,768]{1,2,0:T(8,128)(2,1)S(1)} copy(bf16[1,1536,768]{2,1,0:T(8,128)(2,1)} %param.11) | data formatting | bytes 4718592 | tf_op jit(solution)/shard_map/while | solution.py:103
  2.8 4.3 %copy.18 = bf16[1,1536,768]{1,2,0:T(8,128)(2,1)} copy(bf16[1,1536,768]{2,1,0:T(8,128)(2,1)} %param.12) | data formatting | bytes 4718592 | tf_op jit(solution)/shard_map/while | solution.py:103
  8.7 92.5 %while.18 = (s32[]{:T(128)}, bf16[128,1536]{1,0:T(8,128)(2,1)}, bf16[128,768]{1,0:T(8,128)(2,1)}, bf16[2,128,1536]{2,1,0:T(8,128)(2,1)S(1)}, s32[]{:T(128)}, /*i...) while((s32[]{:T(128)}, bf16[128,1536]{1,0:T(8,128)(2,1)}, ...), condition=%wide.region_7.8_spmd, body=%wide.region_0.7_spmd.sunk | while | flops 1263716864 | bytes 40562208 | solution.py:103
  9.8 13.4 %conditional.2 = ((bf16[128,1536]{1,0:T(8,128)(2,1)S(1)}, bf16[128,768]{1,0:T(8,128)(2,1)})) conditional(s32[]{:T(128)} %convert_element_type.92, (bf16[128,1536]{1,0:T(8,128)(2,1)S(1)}, bf16[128,768]{1,0:T(8,128)(2,1)}) %tuple.47, (bf16[128,1536]{1,0:T(8,128)(2,1)S(1)}, s32[]{:T(128)}, bf16[1,1536,768]{2,1,0:T(8,128)(2,1)}, f32[1]{0:T(128)}, ...), branch_computations={%region_1.1_spmd, %region_2.6_spmd} | conditional | flops 1263323648 | bytes 34663536 | solution.py:91
  14.0 3.0 %broadcast_select_fusion = (bf16[128,768]{1,0:T(8,128)(2,1)}, bf16[128,768]{1,0:T(8,128)(2,1)}) fusion(bf16[128,768]{1,0:T(8,128)(2,1)} %get-tuple-element.250, pred[]{:T(512)S(6)} %eq.19, f32[]{:T(128)S(6)} %sub.9, f32[]{:T(128)} %bitcast.1, bf16[1,1536,768]{2,1,0:T(8,128)(2,1)S(1)} %copy-done.1, bf16[128,1536]{1,0:T(8,128)(2,1)S(1)} %get-tuple-element.246, ...), kind=kOutput, calls=%fused_computation.27 | convolution fusion | flops 303366144 | bytes 3342857 | tf_op jit(solution)/shard_map/while/body/eval_jaxpr/cond/branch_1_fun/dot_general | solution.py:24
  18.8 2.1 %convolution_convert_fusion = bf16[6,128,128]{2,1,0:T(8,128)(2,1)} fusion(bf16[128,6,128]{0,2,1:T(8,128)(2,1)} %bitcast.54, f32[6,128,128]{1,2,0:T(8,128)} %fusion.5), kind=kOutput, calls=%fused_computation.10 | convolution fusion | flops 25461632 | bytes 786432 | tf_op jit(solution)/shard_map/while/body/eval_jaxpr/cond/branch_1_fun/hqk,khd->qhd/dot_general | solution.py:47
  20.9 2.3 %fusion = bf16[128,1536]{1,0:T(8,128)(2,1)S(1)} fusion(bf16[128,768]{0,1:T(8,128)(2,1)} %bitcast.53, bf16[1,768,1536]{2,1,0:T(8,128)(2,1)} %get-tuple-element.253, bf16[128,1536]{1,0:T(8,128)(2,1)S(1)} %get-tuple-element.246), kind=kOutput, calls=%fused_computation.1 | convolution fusion | flops 302579712 | bytes 3342336 | tf_op jit(solution)/shard_map/while/body/eval_jaxpr/cond/branch_1_fun/dot_general | solution.py:24
  23.2 2.0 %collective-permute-start.1 = (bf16[128,768]{1,0:T(8,128)(2,1)}, bf16[128,768]{1,0:T(8,128)(2,1)}, u32[]{:S(2)}, u32[]{:S(2)}) collective-permute-start(bf16[128,768]{1,0:T(8,128)(2,1)} %get-tuple-element.414), channel_id=1, source_target_pairs={{0,16},{1,17},{2,18},{3,19},{4,20},{5,21},{6,22},{7,23},{8,24},{9,... | collective-permute-start | bytes 589832 | tf_op jit(solution)/shard_map/while/body/eval_jaxpr/ppermute | solution.py:16
  25.2 2.0 %collective-permute-start = (bf16[128,1536]{1,0:T(8,128)(2,1)S(1)}, bf16[128,1536]{1,0:T(8,128)(2,1)}, u32[]{:S(2)}, u32[]{:S(2)}) collective-permute-start(bf16[128,1536]{1,0:T(8,128)(2,1)S(1)} %get-tuple-element.413), channel_id=1, source_target_pairs={{0,16},{1,17},{2,18},{3,19},{4,20},{5,21},{6,22},{7,23},{8,24},{9,... | collective-permute-start | bytes 1179656 | tf_op jit(solution)/shard_map/while/body/eval_jaxpr/ppermute | solution.py:16
  27.3 2.8 %collective-permute-done.1 = bf16[128,768]{1,0:T(8,128)(2,1)} collective-permute-done((bf16[128,768]{1,0:T(8,128)(2,1)}, bf16[128,768]{1,0:T(8,128)(2,1)}, u32[]{:S(2)}, u32[]{:S(2)}) %collective-permute-start.1) | collective-permute-done | bytes 196640 | tf_op jit(solution)/shard_map/while/body/eval_jaxpr/ppermute | solution.py:16
  31.7 6.5 %collective-permute-done = bf16[128,1536]{1,0:T(8,128)(2,1)} collective-permute-done((bf16[128,1536]{1,0:T(8,128)(2,1)S(1)}, bf16[128,1536]{1,0:T(8,128)(2,1)}, u32[]{:S(2)}, u32[]{:S(2)}) %collective-permute-start) | collective-permute-done | bytes 393248 | tf_op jit(solution)/shard_map/while/body/eval_jaxpr/ppermute | solution.py:16
  39.3 13.4 %conditional.2 = ((bf16[128,1536]{1,0:T(8,128)(2,1)S(1)}, bf16[128,768]{1,0:T(8,128)(2,1)})) conditional(s32[]{:T(128)} %convert_element_type.92, (bf16[128,1536]{1,0:T(8,128)(2,1)S(1)}, bf16[128,768]{1,0:T(8,128)(2,1)}) %tuple.47, (bf16[128,1536]{1,0:T(8,128)(2,1)S(1)}, s32[]{:T(128)}, bf16[1,1536,768]{2,1,0:T(8,128)(2,1)}, f32[1]{0:T(128)}, ...), branch_computations={%region_1.1_spmd, %region_2.6_spmd} | conditional | flops 1263323648 | bytes 34663536 | solution.py:91
  43.5 3.0 %broadcast_select_fusion = (bf16[128,768]{1,0:T(8,128)(2,1)}, bf16[128,768]{1,0:T(8,128)(2,1)}) fusion(bf16[128,768]{1,0:T(8,128)(2,1)} %get-tuple-element.250, pred[]{:T(512)S(6)} %eq.19, f32[]{:T(128)S(6)} %sub.9, f32[]{:T(128)} %bitcast.1, bf16[1,1536,768]{2,1,0:T(8,128)(2,1)S(1)} %copy-done.1, bf16[128,1536]{1,0:T(8,128)(2,1)S(1)} %get-tuple-element.246, ...), kind=kOutput, calls=%fused_computation.27 | convolution fusion | flops 303366144 | bytes 3342857 | tf_op jit(solution)/shard_map/while/body/eval_jaxpr/cond/branch_1_fun/dot_general | solution.py:24
  48.3 2.1 %convolution_convert_fusion = bf16[6,128,128]{2,1,0:T(8,128)(2,1)} fusion(bf16[128,6,128]{0,2,1:T(8,128)(2,1)} %bitcast.54, f32[6,128,128]{1,2,0:T(8,128)} %fusion.5), kind=kOutput, calls=%fused_computation.10 | convolution fusion | flops 25461632 | bytes 786432 | tf_op jit(solution)/shard_map/while/body/eval_jaxpr/cond/branch_1_fun/hqk,khd->qhd/dot_general | solution.py:47
  50.4 2.3 %fusion = bf16[128,1536]{1,0:T(8,128)(2,1)S(1)} fusion(bf16[128,768]{0,1:T(8,128)(2,1)} %bitcast.53, bf16[1,768,1536]{2,1,0:T(8,128)(2,1)} %get-tuple-element.253, bf16[128,1536]{1,0:T(8,128)(2,1)S(1)} %get-tuple-element.246), kind=kOutput, calls=%fused_computation.1 | convolution fusion | flops 302579712 | bytes 3342336 | tf_op jit(solution)/shard_map/while/body/eval_jaxpr/cond/branch_1_fun/dot_general | solution.py:24
  52.7 5.3 %collective-permute-start.1 = (bf16[128,768]{1,0:T(8,128)(2,1)}, bf16[128,768]{1,0:T(8,128)(2,1)}, u32[]{:S(2)}, u32[]{:S(2)}) collective-permute-start(bf16[128,768]{1,0:T(8,128)(2,1)} %get-tuple-element.414), channel_id=1, source_target_pairs={{0,16},{1,17},{2,18},{3,19},{4,20},{5,21},{6,22},{7,23},{8,24},{9,... | collective-permute-start | bytes 589832 | tf_op jit(solution)/shard_map/while/body/eval_jaxpr/ppermute | solution.py:16
  58.0 2.0 %collective-permute-start = (bf16[128,1536]{1,0:T(8,128)(2,1)S(1)}, bf16[128,1536]{1,0:T(8,128)(2,1)}, u32[]{:S(2)}, u32[]{:S(2)}) collective-permute-start(bf16[128,1536]{1,0:T(8,128)(2,1)S(1)} %get-tuple-element.413), channel_id=1, source_target_pairs={{0,16},{1,17},{2,18},{3,19},{4,20},{5,21},{6,22},{7,23},{8,24},{9,... | collective-permute-start | bytes 1179656 | tf_op jit(solution)/shard_map/while/body/eval_jaxpr/ppermute | solution.py:16
  60.1 2.8 %collective-permute-done.1 = bf16[128,768]{1,0:T(8,128)(2,1)} collective-permute-done((bf16[128,768]{1,0:T(8,128)(2,1)}, bf16[128,768]{1,0:T(8,128)(2,1)}, u32[]{:S(2)}, u32[]{:S(2)}) %collective-permute-start.1) | collective-permute-done | bytes 196640 | tf_op jit(solution)/shard_map/while/body/eval_jaxpr/ppermute | solution.py:16
  64.5 5.6 %collective-permute-done = bf16[128,1536]{1,0:T(8,128)(2,1)} collective-permute-done((bf16[128,1536]{1,0:T(8,128)(2,1)S(1)}, bf16[128,1536]{1,0:T(8,128)(2,1)}, u32[]{:S(2)}, u32[]{:S(2)}) %collective-permute-start) | collective-permute-done | bytes 393248 | tf_op jit(solution)/shard_map/while/body/eval_jaxpr/ppermute | solution.py:16
  71.2 18.7 %collective-permute-start.1 = (bf16[128,768]{1,0:T(8,128)(2,1)}, bf16[128,768]{1,0:T(8,128)(2,1)}, u32[]{:S(2)}, u32[]{:S(2)}) collective-permute-start(bf16[128,768]{1,0:T(8,128)(2,1)} %get-tuple-element.414), channel_id=1, source_target_pairs={{0,16},{1,17},{2,18},{3,19},{4,20},{5,21},{6,22},{7,23},{8,24},{9,... | collective-permute-start | bytes 589832 | tf_op jit(solution)/shard_map/while/body/eval_jaxpr/ppermute | solution.py:16
  89.9 2.0 %collective-permute-start = (bf16[128,1536]{1,0:T(8,128)(2,1)S(1)}, bf16[128,1536]{1,0:T(8,128)(2,1)}, u32[]{:S(2)}, u32[]{:S(2)}) collective-permute-start(bf16[128,1536]{1,0:T(8,128)(2,1)S(1)} %get-tuple-element.413), channel_id=1, source_target_pairs={{0,16},{1,17},{2,18},{3,19},{4,20},{5,21},{6,22},{7,23},{8,24},{9,... | collective-permute-start | bytes 1179656 | tf_op jit(solution)/shard_map/while/body/eval_jaxpr/ppermute | solution.py:16
  92.1 2.8 %collective-permute-done.1 = bf16[128,768]{1,0:T(8,128)(2,1)} collective-permute-done((bf16[128,768]{1,0:T(8,128)(2,1)}, bf16[128,768]{1,0:T(8,128)(2,1)}, u32[]{:S(2)}, u32[]{:S(2)}) %collective-permute-start.1) | collective-permute-done | bytes 196640 | tf_op jit(solution)/shard_map/while/body/eval_jaxpr/ppermute | solution.py:16
  96.5 4.8 %collective-permute-done = bf16[128,1536]{1,0:T(8,128)(2,1)} collective-permute-done((bf16[128,1536]{1,0:T(8,128)(2,1)S(1)}, bf16[128,1536]{1,0:T(8,128)(2,1)}, u32[]{:S(2)}, u32[]{:S(2)}) %collective-permute-start) | collective-permute-done | bytes 393248 | tf_op jit(solution)/shard_map/while/body/eval_jaxpr/ppermute | solution.py:16
  101.2 12.8 %all_to_all.5 = bf16[2,128,1536]{2,1,0:T(8,128)(2,1)S(1)} all-to-all(bf16[2,128,1536]{2,1,0:T(8,128)(2,1)S(1)} %get-tuple-element.271), channel_id=1, replica_groups=mesh['section'=2,'dp'=16] {'section'}, dimensions={0} | all-to-all | bytes 1572864 | tf_op jit(solution)/shard_map/all_to_all | solution.py:106
  (41 shorter events, 21.3 us)
Async XLA Ops:
  10.4 1.7 %copy-start = (bf16[1,1536,768]{1,2,0:T(8,128)(2,1)S(1)}, bf16[1,1536,768]{1,2,0:T(8,128)(2,1)}, u32[]{:S(2)}) copy-start(bf16[1,1536,768]{1,2,0:T(8,128)(2,1)} %get-tuple-element.252) | copy-start | bytes 7077892 | tf_op jit(solution)/shard_map/while/body/eval_jaxpr/cond
  12.1 1.9 %copy-start.1 = (bf16[1,1536,768]{2,1,0:T(8,128)(2,1)S(1)}, bf16[1,1536,768]{2,1,0:T(8,128)(2,1)}, u32[]{:S(2)}) copy-start(bf16[1,1536,768]{2,1,0:T(8,128)(2,1)} %get-tuple-element.248) | copy-start | bytes 7077892 | tf_op jit(solution)/shard_map/while/body/eval_jaxpr/cond
  23.2 6.9 %collective-permute-start.1 = (bf16[128,768]{1,0:T(8,128)(2,1)}, bf16[128,768]{1,0:T(8,128)(2,1)}, u32[]{:S(2)}, u32[]{:S(2)}) collective-permute-start(bf16[128,768]{1,0:T(8,128)(2,1)} %get-tuple-element.414), channel_id=1, source_target_pairs={{0,16},{1,17},{2,18},{3,19},{4,20},{5,21},{6,22},{7,23},{8,24},{9,... | collective-permute-start | bytes 589832 | tf_op jit(solution)/shard_map/while/body/eval_jaxpr/ppermute | solution.py:16
  25.2 13.1 %collective-permute-start = (bf16[128,1536]{1,0:T(8,128)(2,1)S(1)}, bf16[128,1536]{1,0:T(8,128)(2,1)}, u32[]{:S(2)}, u32[]{:S(2)}) collective-permute-start(bf16[128,1536]{1,0:T(8,128)(2,1)S(1)} %get-tuple-element.413), channel_id=1, source_target_pairs={{0,16},{1,17},{2,18},{3,19},{4,20},{5,21},{6,22},{7,23},{8,24},{9,... | collective-permute-start | bytes 1179656 | tf_op jit(solution)/shard_map/while/body/eval_jaxpr/ppermute | solution.py:16
  39.9 1.7 %copy-start = (bf16[1,1536,768]{1,2,0:T(8,128)(2,1)S(1)}, bf16[1,1536,768]{1,2,0:T(8,128)(2,1)}, u32[]{:S(2)}) copy-start(bf16[1,1536,768]{1,2,0:T(8,128)(2,1)} %get-tuple-element.252) | copy-start | bytes 7077892 | tf_op jit(solution)/shard_map/while/body/eval_jaxpr/cond
  41.6 1.9 %copy-start.1 = (bf16[1,1536,768]{2,1,0:T(8,128)(2,1)S(1)}, bf16[1,1536,768]{2,1,0:T(8,128)(2,1)}, u32[]{:S(2)}) copy-start(bf16[1,1536,768]{2,1,0:T(8,128)(2,1)} %get-tuple-element.248) | copy-start | bytes 7077892 | tf_op jit(solution)/shard_map/while/body/eval_jaxpr/cond
  52.7 10.2 %collective-permute-start.1 = (bf16[128,768]{1,0:T(8,128)(2,1)}, bf16[128,768]{1,0:T(8,128)(2,1)}, u32[]{:S(2)}, u32[]{:S(2)}) collective-permute-start(bf16[128,768]{1,0:T(8,128)(2,1)} %get-tuple-element.414), channel_id=1, source_target_pairs={{0,16},{1,17},{2,18},{3,19},{4,20},{5,21},{6,22},{7,23},{8,24},{9,... | collective-permute-start | bytes 589832 | tf_op jit(solution)/shard_map/while/body/eval_jaxpr/ppermute | solution.py:16
  58.0 12.2 %collective-permute-start = (bf16[128,1536]{1,0:T(8,128)(2,1)S(1)}, bf16[128,1536]{1,0:T(8,128)(2,1)}, u32[]{:S(2)}, u32[]{:S(2)}) collective-permute-start(bf16[128,1536]{1,0:T(8,128)(2,1)S(1)} %get-tuple-element.413), channel_id=1, source_target_pairs={{0,16},{1,17},{2,18},{3,19},{4,20},{5,21},{6,22},{7,23},{8,24},{9,... | collective-permute-start | bytes 1179656 | tf_op jit(solution)/shard_map/while/body/eval_jaxpr/ppermute | solution.py:16
  71.2 23.6 %collective-permute-start.1 = (bf16[128,768]{1,0:T(8,128)(2,1)}, bf16[128,768]{1,0:T(8,128)(2,1)}, u32[]{:S(2)}, u32[]{:S(2)}) collective-permute-start(bf16[128,768]{1,0:T(8,128)(2,1)} %get-tuple-element.414), channel_id=1, source_target_pairs={{0,16},{1,17},{2,18},{3,19},{4,20},{5,21},{6,22},{7,23},{8,24},{9,... | collective-permute-start | bytes 589832 | tf_op jit(solution)/shard_map/while/body/eval_jaxpr/ppermute | solution.py:16
  89.9 11.3 %collective-permute-start = (bf16[128,1536]{1,0:T(8,128)(2,1)S(1)}, bf16[128,1536]{1,0:T(8,128)(2,1)}, u32[]{:S(2)}, u32[]{:S(2)}) collective-permute-start(bf16[128,1536]{1,0:T(8,128)(2,1)S(1)} %get-tuple-element.413), channel_id=1, source_target_pairs={{0,16},{1,17},{2,18},{3,19},{4,20},{5,21},{6,22},{7,23},{8,24},{9,... | collective-permute-start | bytes 1179656 | tf_op jit(solution)/shard_map/while/body/eval_jaxpr/ppermute | solution.py:16
where the time goes:
time: 116 us; the launch traced here: 115 us
  starting transfers between devices  32 us (28%)
  waiting for transfers between devices  25.1 us (22%)
  matrix products  20.3 us (18%)
  local copies, waits for them, and re-layouts  19.2 us (17%)
  blocking collectives  12.8 us (11%)
  other arithmetic  3.81 us (3%)
  loops' own time  1.52 us (1%)
    ppermute x6, starting transfers between devices, shifted(): lax.ppermute(value, axis, [(source, source + steps) for source in range(f...  32 us
    ppermute x6, waiting for transfers between devices, shifted(): lax.ppermute(value, axis, [(source, source + steps) for source in range(f...  25.1 us
    dot_general x8, matrix products, project(): return jnp.dot(normed, weight, preferred_element_type=jnp.float32)  14.1 us
    all_to_all x1, blocking collectives, body(): lax.all_to_all(outputs, 'section', split_axis=0, concat_axis=0, tiled=True)  12.8 us
    while x2, local copies, waits for them, and re-layouts, body(): lax.fori_loop(0, step_count, advance, (received, value_store, outputs))  7.13 us
    while x3, local copies, waits for them, and re-layouts  4.93 us
    dot_general x2, matrix products, layer_apply(): jnp.einsum('hqk,khd->qhd', probabilities, used_values, preferred_element_...  4.21 us
    select_n x2, local copies, waits for them, and re-layouts, layer_apply(): jnp.where(first_flag, own_values, blended).reshape(row_count, HEADS, -1)  3.46 us
  transfers between devices with their start and end apart: 6, of which 6 were waited for; matrix products, arithmetic and copies ran while one was open for 5% of the time, Pallas kernels for 0%

commit v1 on v0

v1 whole, which is shorter than its diff:
```python
import functools

import jax
import jax.numpy as jnp
from jax import lax
from jax.experimental import pallas as pl
from jax.experimental.pallas import tpu as pltpu
from jax.sharding import PartitionSpec as P

HEADS = 6

epsilon = 1e-06
score_scale = 0.12
MESH = pl.DeviceIdType.MESH


def norm_rows(tensor):
    return tensor * lax.rsqrt(jnp.mean(tensor * tensor, axis=-1, keepdims=True) + epsilon)


def project(normed, weight):
    return jnp.dot(normed, weight, preferred_element_type=jnp.float32)


def kernel(
    sections,
    inputs_ref,
    wq_hbm,
    wk_hbm,
    wv_hbm,
    wo_hbm,
    mixing_ref,
    out_ref,
    wq,
    wk,
    wv,
    wo,
    h_in,
    h_out,
    v_buf,
    q_buf,
    k_buf,
    used_buf,
    att_buf,
    load_sem,
    hs_sem,
    hr_sem,
    vs_sem,
    vr_sem,
    os_sem,
    or_sem,
    local_sem,
):
    me = lax.axis_index("section")
    last = sections - 1
    micro, rows, width = h_in.shape
    features = v_buf.shape[2]
    head = features // HEADS
    share = micro // sections
    is_first = me == 0
    is_last = me == last

    input_loads = [
        pltpu.make_async_copy(inputs_ref.at[i], h_in.at[i], load_sem.at[4 + i]) for i in range(micro)
    ]
    loads = [
        pltpu.make_async_copy(source.at[0], target, load_sem.at[i])
        for i, (source, target) in enumerate(
            ((wv_hbm, wv), (wq_hbm, wq), (wk_hbm, wk), (wo_hbm, wo))
        )
    ]

    @pl.when(is_first)
    def _():
        input_loads[0].start()

    for load in loads:
        load.start()

    @pl.when(is_first)
    def _():
        for load in input_loads[1:]:
            load.start()

    barrier = pltpu.get_barrier_semaphore()
    for step in range(1, sections):
        pl.semaphore_signal(
            barrier,
            inc=1,
            device_id={"section": lax.rem(me + step, sections)},
            device_id_type=MESH,
        )
    pl.semaphore_wait(barrier, sections - 1)

    onward = jnp.minimum(me + 1, last)

    def h_copy(i):
        return pltpu.make_async_remote_copy(
            src_ref=h_out.at[i],
            dst_ref=h_in.at[i],
            send_sem=hs_sem.at[i],
            recv_sem=hr_sem.at[i],
            device_id={"section": onward},
            device_id_type=MESH,
        )

    def v_copy(i):
        return pltpu.make_async_remote_copy(
            src_ref=v_buf.at[i],
            dst_ref=v_buf.at[i],
            send_sem=vs_sem.at[i],
            recv_sem=vr_sem.at[i],
            device_id={"section": onward},
            device_id_type=MESH,
        )

    def out_copy(i):
        return pltpu.make_async_remote_copy(
            src_ref=h_out.at[i],
            dst_ref=out_ref.at[i % share],
            send_sem=os_sem.at[i],
            recv_sem=or_sem.at[i],
            device_id={"section": i // share},
            device_id_type=MESH,
        )

    def own_copy(i):
        return pltpu.make_async_copy(h_out.at[i], out_ref.at[i % share], local_sem.at[i])

    row_index = lax.broadcasted_iota(jnp.int32, (rows, rows), 0)
    column_index = lax.broadcasted_iota(jnp.int32, (rows, rows), 1)
    causal = row_index >= column_index

    def attend_and_out(i, normed):
        queries = project(normed, wq[...])
        for n in range(HEADS):
            part = slice(n * head, (n + 1) * head)
            q_buf[:, part] = norm_rows(queries[:, part]).astype(jnp.bfloat16)

        def keys_and_rest():
            key_rows = project(normed, wk[...])
            for n in range(HEADS):
                part = slice(n * head, (n + 1) * head)
                k_buf[:, part] = norm_rows(key_rows[:, part]).astype(jnp.bfloat16)
            for n in range(HEADS):
                part = slice(n * head, (n + 1) * head)
                scores = (
                    lax.dot_general(
                        q_buf[:, part],
                        k_buf[:, part],
                        (((1,), (1,)), ((), ())),
                        preferred_element_type=jnp.float32,
                    )
                    * score_scale
                )
                weights = jnp.where(causal, jnp.exp(scores), 0.0)
                probabilities = (weights / jnp.sum(weights, axis=-1, keepdims=True)).astype(
                    jnp.bfloat16
                )
                att_buf[:, part] = project(probabilities, used_buf[:, part]).astype(jnp.bfloat16)

        keys_and_rest()
        added = project(att_buf[...], wo[...])
        h_out[i] = (h_in[i].astype(jnp.float32) + added).astype(jnp.bfloat16)

    @pl.when(is_first)
    def _():
        for i in range(micro):
            input_loads[i].wait()
            normed = norm_rows(h_in[i].astype(jnp.float32)).astype(jnp.bfloat16)
            if i == 0:
                loads[0].wait()
            own = project(normed, wv[...]).astype(jnp.bfloat16)
            v_buf[i] = own
            used_buf[...] = own
            if sections > 1:
                v_copy(i).start()
            if i == 0:
                for load in loads[1:]:
                    load.wait()
            attend_and_out(i, normed)
            if sections > 1:
                h_copy(i).start()
            else:
                own_copy(i).start()

    if sections > 1:

        @pl.when(jnp.logical_not(is_first))
        def _():
            for load in loads:
                load.wait()
            mixing = mixing_ref[0]
            for i in range(micro):
                v_copy(i).wait_recv()
                if sections > 2:

                    @pl.when(jnp.logical_not(is_last))
                    def _():
                        v_copy(i).start()

                h_copy(i).wait_recv()
                normed = norm_rows(h_in[i].astype(jnp.float32)).astype(jnp.bfloat16)
                values = project(normed, wv[...])
                used_buf[...] = (
                    mixing * values + (1.0 - mixing) * v_buf[i].astype(jnp.float32)
                ).astype(jnp.bfloat16)
                attend_and_out(i, normed)

                @pl.when(is_last)
                def _():
                    if i // share == last:
                        own_copy(i).start()
                    else:
                        out_copy(i).start()

                if sections > 2:

                    @pl.when(jnp.logical_not(is_last))
                    def _():
                        h_copy(i).start()

    @pl.when(jnp.logical_not(is_last))
    def _():
        for i in range(micro):
            v_copy(i).wait_send()
            h_copy(i).wait_send()

    for i in range(micro):
        owner = i // share
        if owner == last:

            @pl.when(is_last)
            def _():
                own_copy(i).wait()

        else:

            @pl.when(is_last)
            def _():
                out_copy(i).wait_send()

            @pl.when(me == owner)
            def _():
                out_copy(i).wait_recv()


def body(inputs, w_query, w_key, w_value, w_out, mixing):
    sections = lax.axis_size("section")
    micro, rows, width = inputs.shape
    features = w_value.shape[2]
    share = micro // sections
    bf16 = jnp.bfloat16
    anywhere = pl.BlockSpec(memory_space=pl.ANY)
    dma = pltpu.SemaphoreType.DMA
    return pl.pallas_call(
        functools.partial(kernel, sections),
        out_shape=jax.ShapeDtypeStruct((share, rows, width), bf16),
        in_specs=[anywhere] * 5 + [pl.BlockSpec(memory_space=pltpu.SMEM)],
        out_specs=anywhere,
        scratch_shapes=[
            pltpu.VMEM((width, features), bf16),
            pltpu.VMEM((width, features), bf16),
            pltpu.VMEM((width, features), bf16),
            pltpu.VMEM((features, width), bf16),
            pltpu.VMEM((micro, rows, width), bf16),
            pltpu.VMEM((micro, rows, width), bf16),
            pltpu.VMEM((micro, rows, features), bf16),
            pltpu.VMEM((rows, features), bf16),
            pltpu.VMEM((rows, features), bf16),
            pltpu.VMEM((rows, features), bf16),
            pltpu.VMEM((rows, features), bf16),
            dma((4 + micro,)),
            dma((micro,)),
            dma((micro,)),
            dma((micro,)),
            dma((micro,)),
            dma((micro,)),
            dma((micro,)),
            dma((micro,)),
        ],
        compiler_params=pltpu.CompilerParams(
            collective_id=0, has_side_effects=True, vmem_limit_bytes=60 * 1024 * 1024
        ),
        name="sections",
    )(inputs, w_query, w_key, w_value, w_out, mixing)


def solution(mesh):
    in_specs = (
        P("dp", None, None),
        P("section", None, None),
        P("section", None, None),
        P("section", None, None),
        P("section", None, None),
        P("section"),
    )
    out_specs = P(("dp", "section"), None, None)
    return jax.shard_map(body, mesh=mesh, in_specs=in_specs, out_specs=out_specs, check_vma=False)
```

time: 116 us -> 35.3 us (0.30)
  the two profiles are of different devices: /device:TPU:0 before, /device:TPU:20 now
where the time goes in v1:
time: 35.3 us; the launch traced here: 35.2 us
  Pallas kernels  32.8 us (93%)
  local copies, waits for them, and re-layouts  1.77 us (5%)
  between operations  0.66 us (2%)
    pallas_call x1, Pallas kernels, body(): pl.pallas_call(functools.partial(kernel, sections), out_shape=jax.ShapeDt...  32.8 us
    unnamed x1, local copies, waits for them, and re-layouts  1.77 us

profile of v1, /device:TPU:20, one launch (start us, length us, event | category | flops | bytes accessed | tf_op | source)
XLA Modules:
  0.0 35.2 jit_solution(16251500648371799613)
XLA Ops:
  0.7 32.8 %sections.1 = bf16[1,128,1536]{2,1,0:T(8,128)(2,1)} custom-call(bf16[2,128,1536]{2,1,0:T(8,128)(2,1)} %inputs_ref.1, bf16[1,1536,768]{2,1,0:T(8,128)(2,1)} %wq_hbm.1, bf16[1,1536,768]{2,1,0:T(8,128)(2,1)} %wk_hbm.1, bf16[1,1536,768]{2,1,0:T(8,128)(2,1)} %wv_hbm.1, bf16[1,768,1536]{2,1,0:T(8,128)(2,1)} %wo_hbm.1, f32[1]{0:T(128)S(6)} %copy.8.mixing_ref), custom_call_target="tpu_custom_call" | custom-call | tf_op jit(solution)/shard_map/sections/pallas_call | solution.py:256
  33.4 1.8 %copy.9 = bf16[1,128,1536]{2,1,0:T(8,128)(2,1)} copy(bf16[1,128,1536]{2,1,0:T(8,128)(2,1)} %sections.1) | data formatting | bytes 786432

commit v2 on v1

v2 whole, which is shorter than its diff:
```python
import functools

import jax
import jax.numpy as jnp
from jax import lax
from jax.experimental import pallas as pl
from jax.experimental.pallas import tpu as pltpu
from jax.sharding import PartitionSpec as P

HEADS = 6

epsilon = 1e-06
score_scale = 0.12
MESH = pl.DeviceIdType.MESH


def norm_rows(tensor):
    return tensor * lax.rsqrt(jnp.mean(tensor * tensor, axis=-1, keepdims=True) + epsilon)


def project(normed, weight):
    return jnp.dot(normed, weight, preferred_element_type=jnp.float32)


def kernel(
    sections,
    inputs_ref,
    wq_hbm,
    wk_hbm,
    wv_hbm,
    wo_hbm,
    mixing_ref,
    out_ref,
    wq,
    wk,
    wv,
    wo,
    h_in,
    h_out,
    v_buf,
    q_buf,
    k_buf,
    val_buf,
    p_buf,
    att_buf,
    acc_buf,
    in_sem,
    wv_sem,
    load_sem,
    hs_sem,
    hr_sem,
    vs_sem,
    vr_sem,
    os_sem,
    or_sem,
):
    me = lax.axis_index("section")
    last = sections - 1
    micro, rows, width = h_in.shape
    features = v_buf.shape[2]
    head = features // HEADS
    chunks = HEADS // 2
    span = features // chunks
    share = micro // sections
    is_first = me == 0
    is_last = me == last
    bf16 = jnp.bfloat16
    f32 = jnp.float32

    def head_part(n):
        return slice(n * head, (n + 1) * head)

    def chunk_part(j):
        return slice(j * span, (j + 1) * span)

    def input_load(i):
        return pltpu.make_async_copy(inputs_ref.at[i], h_in.at[i], in_sem.at[i])

    def value_load(j):
        return pltpu.make_async_copy(
            wv_hbm.at[0, :, chunk_part(j)], wv.at[:, chunk_part(j)], wv_sem.at[j]
        )

    loads = [
        pltpu.make_async_copy(source.at[0], target, load_sem.at[i])
        for i, (source, target) in enumerate(((wq_hbm, wq), (wk_hbm, wk), (wo_hbm, wo)))
    ]

    barrier = pltpu.get_barrier_semaphore()
    for step in range(1, sections):
        pl.semaphore_signal(
            barrier,
            inc=1,
            device_id={"section": lax.rem(me + step, sections)},
            device_id_type=MESH,
        )

    @pl.when(is_first)
    def _():
        input_load(0).start()

    for j in range(chunks):
        value_load(j).start()
    for load in loads:
        load.start()

    @pl.when(is_first)
    def _():
        for i in range(1, micro):
            input_load(i).start()

    pl.semaphore_wait(barrier, sections - 1)

    onward = jnp.minimum(me + 1, last)

    def h_copy(i):
        return pltpu.make_async_remote_copy(
            src_ref=h_out.at[i],
            dst_ref=h_in.at[i],
            send_sem=hs_sem.at[i],
            recv_sem=hr_sem.at[i],
            device_id={"section": onward},
            device_id_type=MESH,
        )

    def v_copy(i, j):
        return pltpu.make_async_remote_copy(
            src_ref=v_buf.at[i, :, chunk_part(j)],
            dst_ref=v_buf.at[i, :, chunk_part(j)],
            send_sem=vs_sem.at[i, j],
            recv_sem=vr_sem.at[i, j],
            device_id={"section": onward},
            device_id_type=MESH,
        )

    def out_copy(i):
        return pltpu.make_async_remote_copy(
            src_ref=h_out.at[i],
            dst_ref=out_ref.at[i % share],
            send_sem=os_sem.at[i],
            recv_sem=or_sem.at[i],
            device_id={"section": i // share},
            device_id_type=MESH,
        )

    row_index = lax.broadcasted_iota(jnp.int32, (rows, rows), 0)
    column_index = lax.broadcasted_iota(jnp.int32, (rows, rows), 1)
    causal = row_index >= column_index

    def fill_probabilities(normed):
        queries = project(normed, wq[...])
        key_rows = project(normed, wk[...])
        for n in range(HEADS):
            q_buf[:, head_part(n)] = norm_rows(queries[:, head_part(n)]).astype(bf16)
            k_buf[:, head_part(n)] = norm_rows(key_rows[:, head_part(n)]).astype(bf16)
        for n in range(HEADS):
            scores = (
                lax.dot_general(
                    q_buf[:, head_part(n)],
                    k_buf[:, head_part(n)],
                    (((1,), (1,)), ((), ())),
                    preferred_element_type=f32,
                )
                * score_scale
            )
            weights = jnp.where(causal, jnp.exp(scores), 0.0)
            p_buf[n] = (weights / jnp.sum(weights, axis=-1, keepdims=True)).astype(bf16)

    @pl.when(is_first)
    def _():
        def one(i, carry):
            input_load(i).wait()
            normed = norm_rows(h_in[i].astype(f32)).astype(bf16)
            for j in range(chunks):

                @pl.when(i == 0)
                def _():
                    value_load(j).wait()

                v_buf[i, :, chunk_part(j)] = project(normed, wv[:, chunk_part(j)]).astype(bf16)
                if sections > 1:

                    @pl.when(i == 0)
                    def _():
                        v_copy(i, j).start()

            @pl.when(i == 0)
            def _():
                for load in loads:
                    load.wait()

            fill_probabilities(normed)
            for n in range(HEADS):
                att_buf[:, head_part(n)] = project(p_buf[n], v_buf[i, :, head_part(n)]).astype(bf16)
            result = (h_in[i].astype(f32) + project(att_buf[...], wo[...])).astype(bf16)
            if sections > 1:
                h_out[i] = result
                h_copy(i).start()

                @pl.when(i > 0)
                def _():
                    for j in range(chunks):
                        v_copy(i, j).start()

            else:
                out_ref[i] = result
            return carry

        lax.fori_loop(0, micro, one, 0)

    if sections > 1:

        @pl.when(jnp.logical_not(is_first))
        def _():
            for j in range(chunks):
                value_load(j).wait()
            for load in loads:
                load.wait()
            mixing = mixing_ref[0]

            def one(i, carry):
                h_copy(i).wait_recv()
                normed = norm_rows(h_in[i].astype(f32)).astype(bf16)
                fill_probabilities(normed)
                val_buf[...] = mixing * project(normed, wv[...])
                for j in range(chunks):
                    v_copy(i, j).wait_recv()
                    if sections > 2:

                        @pl.when(jnp.logical_not(is_last))
                        def _():
                            v_copy(i, j).start()

                    used = (
                        val_buf[:, chunk_part(j)]
                        + (1.0 - mixing) * v_buf[i, :, chunk_part(j)].astype(f32)
                    ).astype(bf16)
                    for n in range(2):
                        att_buf[:, head_part(2 * j + n)] = project(
                            p_buf[2 * j + n], used[:, head_part(n)]
                        ).astype(bf16)
                    term = project(att_buf[:, chunk_part(j)], wo[chunk_part(j), :])
                    if j == 0:
                        acc_buf[...] = term
                    elif j < chunks - 1:
                        acc_buf[...] += term
                result = (h_in[i].astype(f32) + (acc_buf[...] + term)).astype(bf16)
                mine = jnp.logical_and(is_last, i // share == last)

                @pl.when(mine)
                def _():
                    out_ref[i % share] = result

                @pl.when(jnp.logical_not(mine))
                def _():
                    h_out[i] = result

                    @pl.when(is_last)
                    def _():
                        out_copy(i).start()

                    if sections > 2:

                        @pl.when(jnp.logical_not(is_last))
                        def _():
                            h_copy(i).start()

                return carry

            lax.fori_loop(0, micro, one, 0)

    @pl.when(jnp.logical_not(is_last))
    def _():
        for i in range(micro):
            for j in range(chunks):
                v_copy(i, j).wait_send()
            h_copy(i).wait_send()

    for i in range(micro):
        if i // share != last:

            @pl.when(is_last)
            def _():
                out_copy(i).wait_send()

            @pl.when(me == i // share)
            def _():
                out_copy(i).wait_recv()


def body(inputs, w_query, w_key, w_value, w_out, mixing):
    sections = lax.axis_size("section")
    micro, rows, width = inputs.shape
    features = w_value.shape[2]
    share = micro // sections
    bf16 = jnp.bfloat16
    anywhere = pl.BlockSpec(memory_space=pltpu.HBM)
    dma = pltpu.SemaphoreType.DMA
    return pl.pallas_call(
        functools.partial(kernel, sections),
        out_shape=pltpu.VMEM((share, rows, width), bf16),
        in_specs=[anywhere] * 5 + [pl.BlockSpec(memory_space=pltpu.SMEM)],
        out_specs=pl.BlockSpec(memory_space=pltpu.VMEM),
        scratch_shapes=[
            pltpu.VMEM((width, features), bf16),
            pltpu.VMEM((width, features), bf16),
            pltpu.VMEM((width, features), bf16),
            pltpu.VMEM((features, width), bf16),
            pltpu.VMEM((micro, rows, width), bf16),
            pltpu.VMEM((micro, rows, width), bf16),
            pltpu.VMEM((micro, rows, features), bf16),
            pltpu.VMEM((rows, features), bf16),
            pltpu.VMEM((rows, features), bf16),
            pltpu.VMEM((rows, features), jnp.float32),
            pltpu.VMEM((HEADS, rows, rows), bf16),
            pltpu.VMEM((rows, features), bf16),
            pltpu.VMEM((rows, width), jnp.float32),
            dma((micro,)),
            dma((HEADS // 2,)),
            dma((3,)),
            dma((micro,)),
            dma((micro,)),
            dma((micro, HEADS // 2)),
            dma((micro, HEADS // 2)),
            dma((micro,)),
            dma((micro,)),
        ],
        compiler_params=pltpu.CompilerParams(
            collective_id=0, has_side_effects=True, vmem_limit_bytes=62 * 1024 * 1024
        ),
        name="sections",
    )(inputs, w_query, w_key, w_value, w_out, mixing)


def solution(mesh):
    in_specs = (
        P("dp", None, None),
        P("section", None, None),
        P("section", None, None),
        P("section", None, None),
        P("section", None, None),
        P("section"),
    )
    out_specs = P(("dp", "section"), None, None)
    return jax.shard_map(body, mesh=mesh, in_specs=in_specs, out_specs=out_specs, check_vma=False)
```

time: 35.3 us -> 31.7 us (0.90)
  the two profiles are of different devices: /device:TPU:20 before, /device:TPU:0 now
where the time goes in v2:
time: 31.7 us; the launch traced here: 31.5 us
  Pallas kernels  30.1 us (95%)
  local copies, waits for them, and re-layouts  0.75 us (2%)
  between operations  0.66 us (2%)
    pallas_call x1, Pallas kernels, body(): pl.pallas_call(functools.partial(kernel, sections), out_shape=pltpu.VMEM(...  30.1 us
    unnamed x1, local copies, waits for them, and re-layouts  0.75 us

profile of v2, /device:TPU:0, one launch (start us, length us, event | category | flops | bytes accessed | tf_op | source)
XLA Modules:
  0.0 31.5 jit_solution(6874963254912575823)
XLA Ops:
  0.7 30.1 %sections.1 = bf16[1,128,1536]{2,1,0:T(8,128)(2,1)S(1)} custom-call(bf16[2,128,1536]{2,1,0:T(8,128)(2,1)} %inputs_ref.1, bf16[1,1536,768]{2,1,0:T(8,128)(2,1)} %wq_hbm.1, bf16[1,1536,768]{2,1,0:T(8,128)(2,1)} %wk_hbm.1, bf16[1,1536,768]{2,1,0:T(8,128)(2,1)} %wv_hbm.1, bf16[1,768,1536]{2,1,0:T(8,128)(2,1)} %wo_hbm.1, f32[1]{0:T(128)S(6)} %copy.9.mixing_ref), custom_call_target="tpu_custom_call" | custom-call | tf_op jit(solution)/shard_map/sections/pallas_call | solution.py:299
  30.8 0.7 %copy.8 = bf16[1,128,1536]{2,1,0:T(8,128)(2,1)} copy(bf16[1,128,1536]{2,1,0:T(8,128)(2,1)S(1)} %sections.1) | data formatting | bytes 786432

commit v3 on v2

--- a/solution.py
+++ b/solution.py
@@ -98,16 +98,16 @@
     @pl.when(is_first)
     def _():
         input_load(0).start()
-
-    for j in range(chunks):
-        value_load(j).start()
-    for load in loads:
-        load.start()
-
-    @pl.when(is_first)
-    def _():
-        for i in range(1, micro):
-            input_load(i).start()
+        value_load(0).start()
+
+    if sections > 1:
+
+        @pl.when(jnp.logical_not(is_first))
+        def _():
+            for j in range(chunks):
+                value_load(j).start()
+            for load in loads:
+                load.start()
 
     pl.semaphore_wait(barrier, sections - 1)
 
@@ -170,12 +170,23 @@
     def _():
         def one(i, carry):
             input_load(i).wait()
+
+            @pl.when(i == 0)
+            def _():
+                for j in range(1, chunks):
+                    value_load(j).start()
+
             normed = norm_rows(h_in[i].astype(f32)).astype(bf16)
             for j in range(chunks):
 
                 @pl.when(i == 0)
                 def _():
                     value_load(j).wait()
+                    if j == 0:
+                        for load in loads:
+                            load.start()
+                        for later in range(1, micro):
+                            input_load(later).start()
 
                 v_buf[i, :, chunk_part(j)] = project(normed, wv[:, chunk_part(j)]).astype(bf16)
                 if sections > 1:

time: 31.7 us -> 32.3 us (1.019)
  Pallas kernels: 30.1 us -> 30.7 us
    pallas_call x1, Pallas kernels: 30.1 us -> 30.7 us  [body(): pl.pallas_call(functools.partial(kernel, sections), out_shape=pltpu.VMEM(...]
where the time goes in v3:
time: 32.3 us; the launch traced here: 32.1 us
  Pallas kernels  30.7 us (95%)
  local copies, waits for them, and re-layouts  0.75 us (2%)
  between operations  0.66 us (2%)
    pallas_call x1, Pallas kernels, body(): pl.pallas_call(functools.partial(kernel, sections), out_shape=pltpu.VMEM(...  30.7 us
    unnamed x1, local copies, waits for them, and re-layouts  0.75 us

profile of v3, /device:TPU:0, one launch (start us, length us, event | category | flops | bytes accessed | tf_op | source)
XLA Modules:
  0.0 32.1 jit_solution(17006579237186244350)
XLA Ops:
  0.7 30.7 %sections.1 = bf16[1,128,1536]{2,1,0:T(8,128)(2,1)S(1)} custom-call(bf16[2,128,1536]{2,1,0:T(8,128)(2,1)} %inputs_ref.1, bf16[1,1536,768]{2,1,0:T(8,128)(2,1)} %wq_hbm.1, bf16[1,1536,768]{2,1,0:T(8,128)(2,1)} %wk_hbm.1, bf16[1,1536,768]{2,1,0:T(8,128)(2,1)} %wv_hbm.1, bf16[1,768,1536]{2,1,0:T(8,128)(2,1)} %wo_hbm.1, f32[1]{0:T(128)S(6)} %copy.9.mixing_ref), custom_call_target="tpu_custom_call" | custom-call | tf_op jit(solution)/shard_map/sections/pallas_call | solution.py:310
  31.4 0.7 %copy.8 = bf16[1,128,1536]{2,1,0:T(8,128)(2,1)} copy(bf16[1,128,1536]{2,1,0:T(8,128)(2,1)S(1)} %sections.1) | data formatting | bytes 786432

commit v4 on v2

--- a/solution.py
+++ b/solution.py
@@ -73,6 +73,9 @@
     def chunk_part(j):
         return slice(j * span, (j + 1) * span)
 
+    def column_part(c):
+        return slice(c * (width // chunks), (c + 1) * (width // chunks))
+
     def input_load(i):
         return pltpu.make_async_copy(inputs_ref.at[i], h_in.at[i], in_sem.at[i])
 
@@ -113,12 +116,12 @@
 
     onward = jnp.minimum(me + 1, last)
 
-    def h_copy(i):
+    def h_copy(i, c):
         return pltpu.make_async_remote_copy(
-            src_ref=h_out.at[i],
-            dst_ref=h_in.at[i],
-            send_sem=hs_sem.at[i],
-            recv_sem=hr_sem.at[i],
+            src_ref=h_out.at[i, :, column_part(c)],
+            dst_ref=h_in.at[i, :, column_part(c)],
+            send_sem=hs_sem.at[i, c],
+            recv_sem=hr_sem.at[i, c],
             device_id={"section": onward},
             device_id_type=MESH,
         )
@@ -133,12 +136,12 @@
             device_id_type=MESH,
         )
 
-    def out_copy(i):
+    def out_copy(i, c):
         return pltpu.make_async_remote_copy(
-            src_ref=h_out.at[i],
-            dst_ref=out_ref.at[i % share],
-            send_sem=os_sem.at[i],
-            recv_sem=or_sem.at[i],
+            src_ref=h_out.at[i, :, column_part(c)],
+            dst_ref=out_ref.at[i % share, :, column_part(c)],
+            send_sem=os_sem.at[i, c],
+            recv_sem=or_sem.at[i, c],
             device_id={"section": i // share},
             device_id_type=MESH,
         )
@@ -192,18 +195,22 @@
             fill_probabilities(normed)
             for n in range(HEADS):
                 att_buf[:, head_part(n)] = project(p_buf[n], v_buf[i, :, head_part(n)]).astype(bf16)
-            result = (h_in[i].astype(f32) + project(att_buf[...], wo[...])).astype(bf16)
+            for c in range(chunks):
+                part = column_part(c)
+                added = project(att_buf[...], wo[:, part])
+                result = (h_in[i, :, part].astype(f32) + added).astype(bf16)
+                if sections > 1:
+                    h_out[i, :, part] = result
+                    h_copy(i, c).start()
+                else:
+                    out_ref[i, :, part] = result
             if sections > 1:
-                h_out[i] = result
-                h_copy(i).start()
 
                 @pl.when(i > 0)
                 def _():
                     for j in range(chunks):
                         v_copy(i, j).start()
 
-            else:
-                out_ref[i] = result
             return carry
 
         lax.fori_loop(0, micro, one, 0)
@@ -219,7 +226,8 @@
             mixing = mixing_ref[0]
 
             def one(i, carry):
-                h_copy(i).wait_recv()
+                for c in range(chunks):
+                    h_copy(i, c).wait_recv()
                 normed = norm_rows(h_in[i].astype(f32)).astype(bf16)
                 fill_probabilities(normed)
                 val_buf[...] = mixing * project(normed, wv[...])
@@ -239,31 +247,35 @@
                         att_buf[:, head_part(2 * j + n)] = project(
                             p_buf[2 * j + n], used[:, head_part(n)]
                         ).astype(bf16)
-                    term = project(att_buf[:, chunk_part(j)], wo[chunk_part(j), :])
-                    if j == 0:
-                        acc_buf[...] = term
-                    elif j < chunks - 1:
-                        acc_buf[...] += term
-                result = (h_in[i].astype(f32) + (acc_buf[...] + term)).astype(bf16)
+                    if j < chunks - 1:
+                        term = project(att_buf[:, chunk_part(j)], wo[chunk_part(j), :])
+                        if j == 0:
+                            acc_buf[...] = term
+                        else:
+                            acc_buf[...] += term
                 mine = jnp.logical_and(is_last, i // share == last)
-
-                @pl.when(mine)
-                def _():
-                    out_ref[i % share] = result
-
-                @pl.when(jnp.logical_not(mine))
-                def _():
-                    h_out[i] = result
-
-                    @pl.when(is_last)
+                for c in range(chunks):
+                    part = column_part(c)
+                    term = project(att_buf[:, chunk_part(chunks - 1)], wo[chunk_part(chunks - 1), part])
+                    result = (h_in[i, :, part].astype(f32) + (acc_buf[:, part] + term)).astype(bf16)
+
+                    @pl.when(mine)
                     def _():
-                        out_copy(i).start()
-
-                    if sections > 2:
-
-                        @pl.when(jnp.logical_not(is_last))
+                        out_ref[i % share, :, part] = result
+
+                    @pl.when(jnp.logical_not(mine))
+                    def _():
+                        h_out[i, :, part] = result
+
+                        @pl.when(is_last)
                         def _():
-                            h_copy(i).start()
+                            out_copy(i, c).start()
+
+                        if sections > 2:
+
+                            @pl.when(jnp.logical_not(is_last))
+                            def _():
+                                h_copy(i, c).start()
 
                 return carry
 
@@ -274,18 +286,20 @@
         for i in range(micro):
             for j in range(chunks):
                 v_copy(i, j).wait_send()
-            h_copy(i).wait_send()
+                h_copy(i, j).wait_send()
 
     for i in range(micro):
         if i // share != last:
 
             @pl.when(is_last)
             def _():
-                out_copy(i).wait_send()
+                for c in range(chunks):
+                    out_copy(i, c).wait_send()
 
             @pl.when(me == i // share)
             def _():
-                out_copy(i).wait_recv()
+                for c in range(chunks):
+                    out_copy(i, c).wait_recv()
 
 
 def body(inputs, w_query, w_key, w_value, w_out, mixing):
@@ -318,12 +332,12 @@
             dma((micro,)),
             dma((HEADS // 2,)),
             dma((3,)),
-            dma((micro,)),
-            dma((micro,)),
-            dma((micro, HEADS // 2)),
-            dma((micro, HEADS // 2)),
-            dma((micro,)),
-            dma((micro,)),
+            dma((micro, HEADS // 2)),
+            dma((micro, HEADS // 2)),
+            dma((micro, HEADS // 2)),
+            dma((micro, HEADS // 2)),
+            dma((micro, HEADS // 2)),
+            dma((micro, HEADS // 2)),
         ],
         compiler_params=pltpu.CompilerParams(
             collective_id=0, has_side_effects=True, vmem_limit_bytes=62 * 1024 * 1024

time: 31.7 us -> 31.7 us (level)
  no operation moved by 1% of the time
where the time goes in v4:
time: 31.7 us; the launch traced here: 31.5 us
  Pallas kernels  30.1 us (95%)
  local copies, waits for them, and re-layouts  0.75 us (2%)
  between operations  0.66 us (2%)
    pallas_call x1, Pallas kernels, body(): pl.pallas_call(functools.partial(kernel, sections), out_shape=pltpu.VMEM(...  30.1 us
    unnamed x1, local copies, waits for them, and re-layouts  0.75 us

profile of v4, /device:TPU:0, one launch (start us, length us, event | category | flops | bytes accessed | tf_op | source)
XLA Modules:
  0.0 31.5 jit_solution(14576179556210936837)
XLA Ops:
  0.7 30.1 %sections.1 = bf16[1,128,1536]{2,1,0:T(8,128)(2,1)S(1)} custom-call(bf16[2,128,1536]{2,1,0:T(8,128)(2,1)} %inputs_ref.1, bf16[1,1536,768]{2,1,0:T(8,128)(2,1)} %wq_hbm.1, bf16[1,1536,768]{2,1,0:T(8,128)(2,1)} %wk_hbm.1, bf16[1,1536,768]{2,1,0:T(8,128)(2,1)} %wv_hbm.1, bf16[1,768,1536]{2,1,0:T(8,128)(2,1)} %wo_hbm.1, f32[1]{0:T(128)S(6)} %copy.9.mixing_ref), custom_call_target="tpu_custom_call" | custom-call | tf_op jit(solution)/shard_map/sections/pallas_call | solution.py:313
  30.7 0.7 %copy.8 = bf16[1,128,1536]{2,1,0:T(8,128)(2,1)} copy(bf16[1,128,1536]{2,1,0:T(8,128)(2,1)S(1)} %sections.1) | data formatting | bytes 786432

commit v5 on v2

--- a/solution.py
+++ b/solution.py
@@ -147,11 +147,14 @@
     column_index = lax.broadcasted_iota(jnp.int32, (rows, rows), 1)
     causal = row_index >= column_index
 
-    def fill_probabilities(normed):
+    def fill_probabilities(normed, arrived):
+        arrived(0)
         queries = project(normed, wq[...])
+        for n in range(HEADS):
+            q_buf[:, head_part(n)] = norm_rows(queries[:, head_part(n)]).astype(bf16)
+        arrived(1)
         key_rows = project(normed, wk[...])
         for n in range(HEADS):
-            q_buf[:, head_part(n)] = norm_rows(queries[:, head_part(n)]).astype(bf16)
             k_buf[:, head_part(n)] = norm_rows(key_rows[:, head_part(n)]).astype(bf16)
         for n in range(HEADS):
             scores = (
@@ -184,14 +187,15 @@
                     def _():
                         v_copy(i, j).start()
 
-            @pl.when(i == 0)
-            def _():
-                for load in loads:
-                    load.wait()
-
-            fill_probabilities(normed)
+            def arrived(which):
+                @pl.when(i == 0)
+                def _():
+                    loads[which].wait()
+
+            fill_probabilities(normed, arrived)
             for n in range(HEADS):
                 att_buf[:, head_part(n)] = project(p_buf[n], v_buf[i, :, head_part(n)]).astype(bf16)
+            arrived(2)
             result = (h_in[i].astype(f32) + project(att_buf[...], wo[...])).astype(bf16)
             if sections > 1:
                 h_out[i] = result
@@ -221,7 +225,7 @@
             def one(i, carry):
                 h_copy(i).wait_recv()
                 normed = norm_rows(h_in[i].astype(f32)).astype(bf16)
-                fill_probabilities(normed)
+                fill_probabilities(normed, lambda which: None)
                 val_buf[...] = mixing * project(normed, wv[...])
                 for j in range(chunks):
                     v_copy(i, j).wait_recv()

time: 31.7 us -> 31.7 us (level)
  no operation moved by 1% of the time
where the time goes in v5:
time: 31.7 us; the launch traced here: 31.6 us
  Pallas kernels  30.1 us (95%)
  local copies, waits for them, and re-layouts  0.75 us (2%)
  between operations  0.66 us (2%)
    pallas_call x1, Pallas kernels, body(): pl.pallas_call(functools.partial(kernel, sections), out_shape=pltpu.VMEM(...  30.1 us
    unnamed x1, local copies, waits for them, and re-layouts  0.75 us

profile of v5, /device:TPU:0, one launch (start us, length us, event | category | flops | bytes accessed | tf_op | source)
XLA Modules:
  0.0 31.6 jit_solution(17921633034814307249)
XLA Ops:
  0.7 30.1 %sections.1 = bf16[1,128,1536]{2,1,0:T(8,128)(2,1)S(1)} custom-call(bf16[2,128,1536]{2,1,0:T(8,128)(2,1)} %inputs_ref.1, bf16[1,1536,768]{2,1,0:T(8,128)(2,1)} %wq_hbm.1, bf16[1,1536,768]{2,1,0:T(8,128)(2,1)} %wk_hbm.1, bf16[1,1536,768]{2,1,0:T(8,128)(2,1)} %wv_hbm.1, bf16[1,768,1536]{2,1,0:T(8,128)(2,1)} %wo_hbm.1, f32[1]{0:T(128)S(6)} %copy.9.mixing_ref), custom_call_target="tpu_custom_call" | custom-call | tf_op jit(solution)/shard_map/sections/pallas_call | solution.py:303
  30.8 0.7 %copy.8 = bf16[1,128,1536]{2,1,0:T(8,128)(2,1)} copy(bf16[1,128,1536]{2,1,0:T(8,128)(2,1)S(1)} %sections.1) | data formatting | bytes 786432

commit v6 on v5

--- a/solution.py
+++ b/solution.py
@@ -67,6 +67,13 @@
     bf16 = jnp.bfloat16
     f32 = jnp.float32
 
+    def over_sequences(one):
+        if micro > 2:
+            lax.fori_loop(0, micro, one, 0)
+        else:
+            for i in range(micro):
+                one(i, 0)
+
     def head_part(n):
         return slice(n * head, (n + 1) * head)
 
@@ -210,7 +217,7 @@
                 out_ref[i] = result
             return carry
 
-        lax.fori_loop(0, micro, one, 0)
+        over_sequences(one)
 
     if sections > 1:
 
@@ -271,7 +278,7 @@
 
                 return carry
 
-            lax.fori_loop(0, micro, one, 0)
+            over_sequences(one)
 
     @pl.when(jnp.logical_not(is_last))
     def _():

time: 31.7 us -> 31.7 us (level)
  no operation moved by 1% of the time
where the time goes in v6:
time: 31.7 us; the launch traced here: 31.5 us
  Pallas kernels  30.1 us (95%)
  local copies, waits for them, and re-layouts  0.75 us (2%)
  between operations  0.66 us (2%)
    pallas_call x1, Pallas kernels, body(): pl.pallas_call(functools.partial(kernel, sections), out_shape=pltpu.VMEM(...  30.1 us
    unnamed x1, local copies, waits for them, and re-layouts  0.75 us

profile of v6, /device:TPU:0, one launch (start us, length us, event | category | flops | bytes accessed | tf_op | source)
XLA Modules:
  0.0 31.5 jit_solution(14266385199229729156)
XLA Ops:
  0.7 30.1 %sections.1 = bf16[1,128,1536]{2,1,0:T(8,128)(2,1)S(1)} custom-call(bf16[2,128,1536]{2,1,0:T(8,128)(2,1)} %inputs_ref.1, bf16[1,1536,768]{2,1,0:T(8,128)(2,1)} %wq_hbm.1, bf16[1,1536,768]{2,1,0:T(8,128)(2,1)} %wk_hbm.1, bf16[1,1536,768]{2,1,0:T(8,128)(2,1)} %wv_hbm.1, bf16[1,768,1536]{2,1,0:T(8,128)(2,1)} %wo_hbm.1, f32[1]{0:T(128)S(6)} %copy.9.mixing_ref), custom_call_target="tpu_custom_call" | custom-call | tf_op jit(solution)/shard_map/sections/pallas_call | solution.py:310
  30.8 0.7 %copy.8 = bf16[1,128,1536]{2,1,0:T(8,128)(2,1)} copy(bf16[1,128,1536]{2,1,0:T(8,128)(2,1)S(1)} %sections.1) | data formatting | bytes 786432
